TPU v7x, 32 devices: a whole 2x2x4 slice. The times are simulated.
32 devices in a mesh: gx: 4 (over z), gy: 2 (over x), gz: 4 (over y, core).
Axes of the slice: x: 2, y: 2, z: 4, core: 2. Of those that a mesh axis runs over, the one named last changes fastest.
Arguments:
- fields_now: float32 [24, 32, 16, 512], P(None, 'gx', 'gy', 'gz'), may hold values from -6 to 6
- parent: float32 [24, 32, 16, 512], P(None, 'gx', 'gy', 'gz'), may hold values from -6 to 6
- advect: float32 [3, 24, 24], replicated, may hold values from -0.75 to 0.75
- diffuse: float32 [3, 24, 24], replicated, may hold values from -0.25 to 0.25
- box_shift: int32 [3], replicated, may hold values from 1 to 4
Outputs:
- section_slope: float32 [24, 32, 16, 512], P(None, 'gx', 'gy', 'gz')
- section_value: float32 [24, 32, 16, 512], P(None, 'gx', 'gy', 'gz')
All inputs are finite; a program needn't handle non-finite values.
Results may differ from a plain program's by a relative error of at most 0.0001.
Values sent between devices are 32-bit elements; how exact they have to be, the bound alone decides.
A program may use at most 64 MiB of HBM per device.

v0:
```python
import jax
import jax.numpy as jnp
from jax import lax
from jax.sharding import PartitionSpec as P

dissipation = 1.0
half_step = 0.125


def shifted(value, axis, by):
    devices = lax.axis_size(axis)
    pairs = [(i, i + by) for i in range(devices) if 0 <= i + by < devices]
    return lax.ppermute(value, axis, pairs)


def padded_2(value, sides, width):
    for axis, dim in sides:
        devices, length = (lax.axis_size(axis), value.shape[dim])
        up = [(i, (i + 1) % devices) for i in range(devices - 1)]
        down = [(j, i) for i, j in up]
        last = lax.slice_in_dim(value, length - width, length, axis=dim)
        initial = lax.slice_in_dim(value, 0, width, axis=dim)
        before = lax.ppermute(last, axis, up)
        after = lax.ppermute(initial, axis, down)
        value = jnp.concatenate([before, value, after], axis=dim)
    return value


def line_terms(padded_line, axis):
    length = padded_line.shape[axis] - 6

    def take_at(offset):
        return lax.slice_in_dim(padded_line, 3 + offset, 3 + offset + length, axis=axis)

    first_diff = (take_at(-2) - 8.0 * take_at(-1) + 8.0 * take_at(1) - take_at(2)) / 12.0
    second_diff = (
        -take_at(-2) + 16.0 * take_at(-1) - 30.0 * take_at(0) + 16.0 * take_at(1) - take_at(2)
    ) / 12.0
    sixth_diff = (
        take_at(-3)
        - 6.0 * take_at(-2)
        + 15.0 * take_at(-1)
        - 20.0 * take_at(0)
        + 15.0 * take_at(1)
        - 6.0 * take_at(2)
        + take_at(3)
    )
    return (first_diff, second_diff, sixth_diff)


def mix_fields(matrix, field):
    flat = field.reshape(field.shape[0], -1)
    return jnp.dot(
        matrix, flat, precision=lax.Precision.HIGHEST, preferred_element_type=jnp.float32
    ).reshape(field.shape)


def center_crop(padded, axis):
    window = [slice(None)] * 4
    for other in (1, 2, 3):
        if other != axis:
            window[other] = slice(3, padded.shape[other] - 3)
    return padded[tuple(window)]


def axis_terms(line, axis, advect, diffuse):
    first_diff, second_diff, sixth_diff = line_terms(line, axis)
    coupled = mix_fields(advect[axis - 1], first_diff) + mix_fields(diffuse[axis - 1], second_diff)
    return (coupled, sixth_diff)


def whole_terms(padded, advect, diffuse):
    linear, smooth = axis_terms(center_crop(padded, 1), 1, advect, diffuse)
    for axis in (2, 3):
        coupled, sixth_diff = axis_terms(center_crop(padded, axis), axis, advect, diffuse)
        linear = linear + coupled
        smooth = smooth + sixth_diff
    return (linear, smooth)


def finish(new_box, linear, smooth):
    lapse_factor = 1.0 + 0.25 * jnp.tanh(new_box[0])
    section_slope = lapse_factor * linear + dissipation / 64.0 * smooth
    section_value = new_box + half_step * section_slope
    return (section_slope, section_value)


def box_cells(lengths, block, offset):
    rows_x = (
        lax.axis_index("gx") * block[0]
        - offset
        + lax.broadcasted_iota(jnp.int32, (1, lengths[0], 1, 1), 1)
    )
    rows_y = (
        lax.axis_index("gy") * block[1]
        - offset
        + lax.broadcasted_iota(jnp.int32, (1, 1, lengths[1], 1), 2)
    )
    rows_z = (
        lax.axis_index("gz") * block[2]
        - offset
        + lax.broadcasted_iota(jnp.int32, (1, 1, 1, lengths[2]), 3)
    )
    totals = (
        block[0] * lax.axis_size("gx"),
        block[1] * lax.axis_size("gy"),
        block[2] * lax.axis_size("gz"),
    )
    return ((rows_x, rows_y, rows_z), totals)


def from_old_mask(cells, totals, box_shift):
    return (
        (cells[0] + box_shift[0] < totals[0])
        & (cells[1] + box_shift[1] < totals[1])
        & (cells[2] + box_shift[2] < totals[2])
    )


def local(fields_now, parent, advect, diffuse, box_shift):
    count_f, count_x, count_y, count_z = fields_now.shape
    block = (count_x, count_y, count_z)
    anchor = jnp.zeros((), jnp.int32)
    from_above = shifted(fields_now[:, :4], "gx", -1)
    extended = jnp.concatenate([fields_now, from_above], axis=1)
    from_above = shifted(extended[:, :, :4], "gy", -1)
    extended = jnp.concatenate([extended, from_above], axis=2)
    from_above = shifted(extended[:, :, :, :4], "gz", -1)
    extended = jnp.concatenate([extended, from_above], axis=3)
    moved_cells = lax.dynamic_slice(
        extended, (anchor, box_shift[0], box_shift[1], box_shift[2]), fields_now.shape
    )
    cells, totals = box_cells(block, block, 0)
    new_box = jnp.where(from_old_mask(cells, totals, box_shift), moved_cells, parent)
    padded = padded_2(new_box, (("gx", 1), ("gy", 2), ("gz", 3)), 3)
    linear, smooth = whole_terms(padded, advect, diffuse)
    return finish(new_box, linear, smooth)


def solution(mesh):
    return jax.shard_map(
        local,
        mesh=mesh,
        in_specs=(P(None, "gx", "gy", "gz"), P(None, "gx", "gy", "gz"), P(), P(), P()),
        out_specs=(P(None, "gx", "gy", "gz"), P(None, "gx", "gy", "gz")),
        check_vma=False,
    )
```

profile of v0, /device:TPU:0, one launch (start us, length us, event | category | flops | bytes accessed | tf_op | source)
XLA Modules:
  0.0 122.9 jit_solution(6595532429708888089)
XLA Ops:
  0.6 1.1 slice.216
  1.7 0.2 copy.73
  2.0 0.0 copy-start.16
  2.0 1.3 %collective-permute-start = (f32[24,4,8,128]{3,0,2,1:T(8,128)S(1)}, f32[24,4,8,128]{3,0,2,1:T(8,128)S(1)}, u32[]{:S(2)}, u32[]{:S(2)}) collective-permute-start(f32[24,4,8,128]{3,0,2,1:T(8,128)S(1)} %copy.73), channel_id=1, source_target_pairs={{8,0},{16,8},{24,16},{9,1},{17,9},{25,17},{10,2},{18,10},{26,18},{... | collective-permute-start | bytes 1179656 | tf_op jit(solution)/shard_map/ppermute | solution.py:13
  3.3 0.5 constant_dynamic-update-slice_fusion.1
  3.8 12.3 %collective-permute-done = f32[24,4,8,128]{3,0,2,1:T(8,128)S(1)} collective-permute-done((f32[24,4,8,128]{3,0,2,1:T(8,128)S(1)}, f32[24,4,8,128]{3,0,2,1:T(8,128)S(1)}, u32[]{:S(2)}, u32[]{:S(2)}) %collective-permute-start) | collective-permute-done | bytes 393248 | tf_op jit(solution)/shard_map/ppermute | solution.py:13
  16.1 1.3 %collective-permute-start.1 = (f32[24,12,4,128]{3,0,2,1:T(8,128)S(1)}, f32[24,12,4,128]{3,0,2,1:T(8,128)S(1)}, u32[]{:S(2)}, u32[]{:S(2)}) collective-permute-start(f32[24,12,4,128]{3,0,2,1:T(8,128)S(1)} %slice.217), channel_id=1, source_target_pairs={{4,0},{5,1},{6,2},{7,3},{12,8},{13,9},{14,10},{15,11},{20,16},{21,... | collective-permute-start | bytes 1769480 | tf_op jit(solution)/shard_map/ppermute | solution.py:13
  17.5 0.6 fusion.61
  18.1 0.7 add_compare_fusion
  18.7 1.3 %add_compare_fusion.1 = (pred[8]{0:T(512)(128)(4,1)S(1)}, pred[8]{0:T(512)(128)(4,1)S(1)}) fusion(s32[]{:T(128)} %bitcast.1, s32[]{:T(128)S(6)} %mul.121, s32[]{:T(128)} %bitcast, s32[]{:T(128)S(6)} %mul.120), kind=kLoop, calls=%fused_computation.112 | loop fusion | flops 48 | bytes 32 | tf_op jit(solution)/shard_map/lt | solution.py:115
  20.0 0.1 broadcast_and_fusion.1
  20.1 12.5 %collective-permute-done.1 = f32[24,12,4,128]{3,0,2,1:T(8,128)S(1)} collective-permute-done((f32[24,12,4,128]{3,0,2,1:T(8,128)S(1)}, f32[24,12,4,128]{3,0,2,1:T(8,128)S(1)}, u32[]{:S(2)}, u32[]{:S(2)}) %collective-permute-start.1) | collective-permute-done | bytes 589856 | tf_op jit(solution)/shard_map/ppermute | solution.py:13
  32.5 1.4 %pad_maximum_fusion.2 = f32[24,12,12,4]{3,0,2,1:T(8,128)} fusion(f32[24,12,4,128]{3,0,2,1:T(8,128)S(1)} %collective-permute-done.1, f32[24,12,8,128]{3,0,2,1:T(8,128)S(1)} %constant_dynamic-update-slice_fusion), kind=kLoop, calls=%fused_computation.11 | loop fusion | flops 13824 | bytes 1824768 | tf_op jit(solution)/shard_map/concatenate | solution.py:127
  33.9 2.8 %copy.21 = f32[24,12,12,4]{0,2,3,1:T(8,128)S(1)} copy(f32[24,12,12,4]{3,0,2,1:T(8,128)} %pad_maximum_fusion.2) | data formatting | bytes 110592 | tf_op jit(solution)/shard_map/slice | solution.py:128
  36.7 1.3 %collective-permute-start.2 = (f32[24,12,12,4]{0,2,3,1:T(8,128)S(1)}, f32[24,12,12,4]{0,2,3,1:T(8,128)S(1)}, u32[]{:S(2)}, u32[]{:S(2)}) collective-permute-start(f32[24,12,12,4]{0,2,3,1:T(8,128)S(1)} %copy.21), channel_id=1, source_target_pairs={{1,0},{2,1},{3,2},{5,4},{6,5},{7,6},{9,8},{10,9},{11,10},{13,12},{... | collective-permute-start | bytes 165896 | tf_op jit(solution)/shard_map/ppermute | solution.py:13
  38.0 0.1 broadcast_and_fusion
  43.8 0.0 collective-permute-done.2
  43.8 2.2 %copy.22 = f32[24,12,12,4]{3,0,2,1:T(8,128)} copy(f32[24,12,12,4]{0,2,3,1:T(8,128)S(1)} %collective-permute-done.2) | data formatting | bytes 110592 | tf_op jit(solution)/shard_map/ppermute | solution.py:13
  46.0 1.9 %fusion.9 = f32[24,8,8,128]{3,0,2,1:T(8,128)S(1)} fusion(s32[]{:T(128)S(6)} %select_n.13, s32[]{:T(128)S(6)} %select_n.14, s32[]{:T(128)S(6)} %select_n.15, f32[24,12,8,128]{3,0,2,1:T(8,128)S(1)} %constant_dynamic-update-slice_fusion, f32[24,12,4,128]{3,0,2,1:T(8,128)S(1)} %collective-permute-done.1, f32[24,12,12,4]{3,0,2,1:T(8,128)} %copy.22, ...), kind=kLoop, calls=%fused_computation.27 | loop fusion | flops 589824 | bytes 3405836 | tf_op jit(solution)/shard_map/jit(_where)/select_n | solution.py:134
  48.0 3.4 %collective-permute-start.3 = (f32[24,3,8,128]{3,0,2,1:T(8,128)S(1)}, f32[24,3,8,128]{3,0,2,1:T(8,128)S(1)}, u32[]{:S(2)}, u32[]{:S(2)}) collective-permute-start(f32[24,3,8,128]{3,0,2,1:T(8,128)S(1)} %get-tuple-element.25), channel_id=1, source_target_pairs={{0,8},{8,16},{16,24},{1,9},{9,17},{17,25},{2,10},{10,18},{18,26},{... | collective-permute-start | bytes 884744 | tf_op jit(solution)/shard_map/ppermute | solution.py:23
  51.4 1.3 %collective-permute-start.4 = (f32[24,3,8,128]{3,0,2,1:T(8,128)S(1)}, f32[24,3,8,128]{3,0,2,1:T(8,128)S(1)}, u32[]{:S(2)}, u32[]{:S(2)}) collective-permute-start(f32[24,3,8,128]{3,0,2,1:T(8,128)S(1)} %get-tuple-element.26), channel_id=1, source_target_pairs={{8,0},{16,8},{24,16},{9,1},{17,9},{25,17},{10,2},{18,10},{26,18},{... | collective-permute-start | bytes 884744 | tf_op jit(solution)/shard_map/ppermute | solution.py:24
  52.7 5.1 %collective-permute-done.3 = f32[24,3,8,128]{3,0,2,1:T(8,128)S(1)} collective-permute-done((f32[24,3,8,128]{3,0,2,1:T(8,128)S(1)}, f32[24,3,8,128]{3,0,2,1:T(8,128)S(1)}, u32[]{:S(2)}, u32[]{:S(2)}) %collective-permute-start.3) | collective-permute-done | bytes 294944 | tf_op jit(solution)/shard_map/ppermute | solution.py:23
  57.8 4.7 %collective-permute-done.4 = f32[24,3,8,128]{3,0,2,1:T(8,128)S(1)} collective-permute-done((f32[24,3,8,128]{3,0,2,1:T(8,128)S(1)}, f32[24,3,8,128]{3,0,2,1:T(8,128)S(1)}, u32[]{:S(2)}, u32[]{:S(2)}) %collective-permute-start.4) | collective-permute-done | bytes 294944 | tf_op jit(solution)/shard_map/ppermute | solution.py:24
  62.5 0.1 pad_maximum_fusion.21
  62.6 1.5 %collective-permute-start.5 = (f32[24,14,3,128]{3,0,2,1:T(8,128)S(1)}, f32[24,14,3,128]{3,0,2,1:T(8,128)S(1)}, u32[]{:S(2)}, u32[]{:S(2)}) collective-permute-start(f32[24,14,3,128]{3,0,2,1:T(8,128)S(1)} %get-tuple-element.21), channel_id=1, source_target_pairs={{0,4},{1,5},{2,6},{3,7},{8,12},{9,13},{10,14},{11,15},{16,20},{17,... | collective-permute-start | bytes 1548296 | tf_op jit(solution)/shard_map/ppermute | solution.py:23
  64.0 1.3 %collective-permute-start.6 = (f32[24,14,3,128]{3,0,2,1:T(8,128)S(1)}, f32[24,14,3,128]{3,0,2,1:T(8,128)S(1)}, u32[]{:S(2)}, u32[]{:S(2)}) collective-permute-start(f32[24,14,3,128]{3,0,2,1:T(8,128)S(1)} %get-tuple-element.22), channel_id=1, source_target_pairs={{4,0},{5,1},{6,2},{7,3},{12,8},{13,9},{14,10},{15,11},{20,16},{21,... | collective-permute-start | bytes 1548296 | tf_op jit(solution)/shard_map/ppermute | solution.py:24
  65.4 10.4 %collective-permute-done.5 = f32[24,14,3,128]{3,0,2,1:T(8,128)S(1)} collective-permute-done((f32[24,14,3,128]{3,0,2,1:T(8,128)S(1)}, f32[24,14,3,128]{3,0,2,1:T(8,128)S(1)}, u32[]{:S(2)}, u32[]{:S(2)}) %collective-permute-start.5) | collective-permute-done | bytes 516128 | tf_op jit(solution)/shard_map/ppermute | solution.py:23
  75.8 4.1 %collective-permute-done.6 = f32[24,14,3,128]{3,0,2,1:T(8,128)S(1)} collective-permute-done((f32[24,14,3,128]{3,0,2,1:T(8,128)S(1)}, f32[24,14,3,128]{3,0,2,1:T(8,128)S(1)}, u32[]{:S(2)}, u32[]{:S(2)}) %collective-permute-start.6) | collective-permute-done | bytes 516128 | tf_op jit(solution)/shard_map/ppermute | solution.py:24
  79.9 0.2 pad_maximum_fusion
  80.1 2.9 %fusion.59 = (f32[24,14,14,3]{3,0,2,1:T(8,128)}, f32[24,14,14,3]{3,0,2,1:T(8,128)}) fusion(f32[24,14,14,128]{3,0,2,1:T(8,128)S(1)} %pad_maximum_fusion), kind=kLoop, calls=%fused_computation.114 | loop fusion | bytes 225792 | tf_op jit(solution)/shard_map/slice | solution.py:21
  83.0 3.2 %copy.28 = f32[24,14,14,3]{0,2,3,1:T(8,128)S(1)} copy(f32[24,14,14,3]{3,0,2,1:T(8,128)} %get-tuple-element.15) | data formatting | bytes 112896 | tf_op jit(solution)/shard_map/slice | solution.py:21
  86.2 3.9 %copy.30 = f32[24,14,14,3]{0,2,3,1:T(8,128)} copy(f32[24,14,14,3]{3,0,2,1:T(8,128)} %get-tuple-element.16) | data formatting | bytes 112896 | tf_op jit(solution)/shard_map/slice | solution.py:22
  90.1 1.3 %collective-permute-start.8 = (f32[24,14,14,3]{0,2,3,1:T(8,128)}, f32[24,14,14,3]{0,2,3,1:T(8,128)}, u32[]{:S(2)}, u32[]{:S(2)}) collective-permute-start(f32[24,14,14,3]{0,2,3,1:T(8,128)} %copy.30), channel_id=1, source_target_pairs={{1,0},{2,1},{3,2},{5,4},{6,5},{7,6},{9,8},{10,9},{11,10},{13,12},{... | collective-permute-start | bytes 169352 | tf_op jit(solution)/shard_map/ppermute | solution.py:24
  91.4 3.8 %collective-permute-start.7 = (f32[24,14,14,3]{0,2,3,1:T(8,128)S(1)}, f32[24,14,14,3]{0,2,3,1:T(8,128)}, u32[]{:S(2)}, u32[]{:S(2)}) collective-permute-start(f32[24,14,14,3]{0,2,3,1:T(8,128)S(1)} %copy.28), channel_id=1, source_target_pairs={{0,1},{1,2},{2,3},{4,5},{5,6},{6,7},{8,9},{9,10},{10,11},{12,13},{... | collective-permute-start | bytes 169352 | tf_op jit(solution)/shard_map/ppermute | solution.py:23
  95.1 0.2 maximum_maximum_fusion
  95.4 1.1 subtract_multiply_fusion.2
  96.5 0.1 copy-done.1
  96.7 0.6 copy-done.3
  97.3 0.2 copy.27
  97.5 0.0 copy-start.14
  97.5 0.2 copy.26
  97.6 0.2 copy.24
  97.8 0.4 copy-done.14
  98.2 1.2 %fusion.17 = f32[8192,24]{0,1:T(8,128)S(1)} fusion(f32[3,8,64,128]{3,2,1,0:T(8,128)S(1)} %bitcast.58, f32[3,24,24]{2,1,0:T(8,128)S(1)} %copy-done.14), kind=kOutput, calls=%fused_computation.35 | convolution fusion | flops 56623104 | bytes 1585152 | tf_op jit(solution)/shard_map/dot_general | solution.py:53
  99.5 0.0 copy-start.15
  99.5 1.3 %fusion.22 = f32[8192,24]{0,1:T(8,128)S(1)} fusion(f32[3,8,64,128]{3,2,1,0:T(8,128)S(1)} %bitcast.59, f32[3,24,24]{2,1,0:T(8,128)S(1)} %copy-done.14), kind=kOutput, calls=%fused_computation.40 | convolution fusion | flops 56623104 | bytes 1585152 | tf_op jit(solution)/shard_map/dot_general | solution.py:53
  100.8 0.2 copy.25
  100.9 1.3 %convolution_add_fusion.2 = f32[8192,24]{0,1:T(8,128)S(1)} fusion(f32[8192,24]{0,1:T(8,128)S(1)} %fusion.22, f32[3,8,64,128]{3,2,1,0:T(8,128)S(1)} %bitcast.63, f32[3,24,24]{2,1,0:T(8,128)S(1)} %copy-done.15), kind=kOutput, calls=%fused_computation.4 | convolution fusion | flops 56819712 | bytes 2371584 | tf_op jit(solution)/shard_map/dot_general | solution.py:53
  102.2 2.1 %fusion.1 = f32[8192,24]{0,1:T(8,128)} fusion(f32[8192,24]{0,1:T(8,128)S(1)} %convolution_add_fusion.2, f32[8192,24]{0,1:T(8,128)S(1)} %fusion.17, f32[3,8,64,128]{3,2,1,0:T(8,128)S(1)} %bitcast.61, f32[3,24,24]{2,1,0:T(8,128)S(1)} %copy-done.15), kind=kOutput, calls=%fused_computation.3 | convolution fusion | flops 57016320 | bytes 3158016 | tf_op jit(solution)/shard_map/dot_general | solution.py:53
  104.3 0.0 collective-permute-done.7
  104.4 2.2 %copy.29 = f32[24,14,14,3]{3,0,2,1:T(8,128)S(1)} copy(f32[24,14,14,3]{0,2,3,1:T(8,128)} %collective-permute-done.7) | data formatting | bytes 112896 | tf_op jit(solution)/shard_map/ppermute | solution.py:23
  106.5 3.6 %copy.31 = f32[24,14,14,3]{3,0,2,1:T(8,128)} copy(f32[24,14,14,3]{0,2,3,1:T(8,128)} %collective-permute-done.8) | data formatting | bytes 112896 | tf_op jit(solution)/shard_map/ppermute | solution.py:24
  110.2 3.1 %subtract_multiply_fusion = (f32[24,8,8,128]{3,0,2,1:T(8,128)S(1)}, f32[24,8,8,128]{3,0,2,1:T(8,128)S(1)}, f32[24,8,8,128]{3,0,2,1:T(8,128)S(1)}, f32[24,8,8,128]{3,0,2,1:T(8,128)S(1)}, f32[24,8,8,128]{3,0,2,1:T(8,128)S(1)}) fusion(f32[24,8,8,128]{3,0,2,1:T(8,128)S(1)} %fusion.9, f32[24,14,3,128]{3,0,2,1:T(8,128)} %copy-done.9, ...), kind=kLoop, calls=%fused_computation.83 | loop fusion | flops 5701632 | bytes 6453504 | tf_op jit(solution)/shard_map/div | solution.py:36
  113.3 0.2 copy.33
  113.5 0.0 copy-start.11
  113.5 0.2 subtract_multiply_fusion.1
  113.7 0.0 copy-start.10
  113.7 0.2 copy.32
  113.9 2.1 %fusion.12 = f32[8192,24]{0,1:T(8,128)S(1)} fusion(f32[3,8,64,128]{3,2,1,0:T(8,128)S(1)} %bitcast.60, f32[3,24,24]{2,1,0:T(8,128)} %param.7), kind=kOutput, calls=%fused_computation.30 | convolution fusion | flops 56623104 | bytes 1585152 | tf_op jit(solution)/shard_map/dot_general | solution.py:53
  116.0 2.2 %fusion.2 = f32[3,8,64,128]{3,1,2,0:T(8,128)S(1)} fusion(f32[8192,24]{0,1:T(8,128)S(1)} %copy-done.11, f32[8192,24]{0,1:T(8,128)S(1)} %fusion.12, f32[3,8,64,128]{3,2,1,0:T(8,128)S(1)} %bitcast.62, f32[3,24,24]{2,1,0:T(8,128)} %param.8), kind=kOutput, calls=%fused_computation.16 | convolution fusion | flops 57016320 | bytes 3158016 | tf_op jit(solution)/shard_map/dot_general | solution.py:53
  118.2 0.1 copy.43
  118.4 2.4 %multiply_add_fusion = (f32[24,8,8,128]{3,0,2,1:T(8,128)S(1)}, f32[24,8,8,128]{3,0,2,1:T(8,128)S(1)}) fusion(f32[24,8,8,128]{3,0,2,1:T(8,128)S(1)} %fusion.9, f32[24,14,14,3]{3,0,2,1:T(8,128)S(1)} %copy-done, f32[24,14,3,128]{3,0,2,1:T(8,128)S(1)} %copy-done.10, f32[24,3,8,128]{3,0,2,1:T(8,128)S(1)} %copy-done.6, ...), kind=kLoop, calls=%fused_computation.82 | loop fusion | flops 10616832 | bytes 12777728 | tf_op jit(solution)/shard_map/add | solution.py:84
  120.8 1.0 copy.36
  121.8 1.0 copy.35
  (31 shorter events, 0.2 us)
Async XLA Ops:
  0.6 2.7 %copy-start.12 = (f32[24,8,8,128]{3,2,1,0:T(8,128)S(1)}, f32[24,8,8,128]{3,2,1,0:T(8,128)}, u32[]{:S(2)}) copy-start(f32[24,8,8,128]{3,2,1,0:T(8,128)} %param.5) | copy-start | bytes 2359300
  2.0 15.5 %copy-start.16 = (s32[3]{0:T(128)S(1)}, s32[3]{0:T(128)}, u32[]{:S(2)}) copy-start(s32[3]{0:T(128)} %param.9) | copy-start | bytes 40
  2.0 14.1 %collective-permute-start = (f32[24,4,8,128]{3,0,2,1:T(8,128)S(1)}, f32[24,4,8,128]{3,0,2,1:T(8,128)S(1)}, u32[]{:S(2)}, u32[]{:S(2)}) collective-permute-start(f32[24,4,8,128]{3,0,2,1:T(8,128)S(1)} %copy.73), channel_id=1, source_target_pairs={{8,0},{16,8},{24,16},{9,1},{17,9},{25,17},{10,2},{18,10},{26,18},{... | collective-permute-start | bytes 1179656 | tf_op jit(solution)/shard_map/ppermute | solution.py:13
  16.1 16.4 %collective-permute-start.1 = (f32[24,12,4,128]{3,0,2,1:T(8,128)S(1)}, f32[24,12,4,128]{3,0,2,1:T(8,128)S(1)}, u32[]{:S(2)}, u32[]{:S(2)}) collective-permute-start(f32[24,12,4,128]{3,0,2,1:T(8,128)S(1)} %slice.217), channel_id=1, source_target_pairs={{4,0},{5,1},{6,2},{7,3},{12,8},{13,9},{14,10},{15,11},{20,16},{21,... | collective-permute-start | bytes 1769480 | tf_op jit(solution)/shard_map/ppermute | solution.py:13
  33.9 12.1 %copy-start.13 = (f32[24,8,8,128]{3,2,1,0:T(8,128)S(1)}, f32[24,8,8,128]{3,2,1,0:T(8,128)}, u32[]{:S(2)}) copy-start(f32[24,8,8,128]{3,2,1,0:T(8,128)} %param.6) | copy-start | bytes 2359300
  36.7 7.1 %collective-permute-start.2 = (f32[24,12,12,4]{0,2,3,1:T(8,128)S(1)}, f32[24,12,12,4]{0,2,3,1:T(8,128)S(1)}, u32[]{:S(2)}, u32[]{:S(2)}) collective-permute-start(f32[24,12,12,4]{0,2,3,1:T(8,128)S(1)} %copy.21), channel_id=1, source_target_pairs={{1,0},{2,1},{3,2},{5,4},{6,5},{7,6},{9,8},{10,9},{11,10},{13,12},{... | collective-permute-start | bytes 165896 | tf_op jit(solution)/shard_map/ppermute | solution.py:13
  48.0 9.8 %collective-permute-start.3 = (f32[24,3,8,128]{3,0,2,1:T(8,128)S(1)}, f32[24,3,8,128]{3,0,2,1:T(8,128)S(1)}, u32[]{:S(2)}, u32[]{:S(2)}) collective-permute-start(f32[24,3,8,128]{3,0,2,1:T(8,128)S(1)} %get-tuple-element.25), channel_id=1, source_target_pairs={{0,8},{8,16},{16,24},{1,9},{9,17},{17,25},{2,10},{10,18},{18,26},{... | collective-permute-start | bytes 884744 | tf_op jit(solution)/shard_map/ppermute | solution.py:23
  51.4 11.1 %collective-permute-start.4 = (f32[24,3,8,128]{3,0,2,1:T(8,128)S(1)}, f32[24,3,8,128]{3,0,2,1:T(8,128)S(1)}, u32[]{:S(2)}, u32[]{:S(2)}) collective-permute-start(f32[24,3,8,128]{3,0,2,1:T(8,128)S(1)} %get-tuple-element.26), channel_id=1, source_target_pairs={{8,0},{16,8},{24,16},{9,1},{17,9},{25,17},{10,2},{18,10},{26,18},{... | collective-permute-start | bytes 884744 | tf_op jit(solution)/shard_map/ppermute | solution.py:24
  62.5 32.9 %copy-start.5 = (f32[24,3,8,128]{3,0,2,1:T(8,128)}, f32[24,3,8,128]{3,0,2,1:T(8,128)S(1)}, u32[]{:S(2)}) copy-start(f32[24,3,8,128]{3,0,2,1:T(8,128)S(1)} %collective-permute-done.4) | copy-start | bytes 884740
  62.6 13.2 %collective-permute-start.5 = (f32[24,14,3,128]{3,0,2,1:T(8,128)S(1)}, f32[24,14,3,128]{3,0,2,1:T(8,128)S(1)}, u32[]{:S(2)}, u32[]{:S(2)}) collective-permute-start(f32[24,14,3,128]{3,0,2,1:T(8,128)S(1)} %get-tuple-element.21), channel_id=1, source_target_pairs={{0,4},{1,5},{2,6},{3,7},{8,12},{9,13},{10,14},{11,15},{16,20},{17,... | collective-permute-start | bytes 1548296 | tf_op jit(solution)/shard_map/ppermute | solution.py:23
  64.0 15.9 %collective-permute-start.6 = (f32[24,14,3,128]{3,0,2,1:T(8,128)S(1)}, f32[24,14,3,128]{3,0,2,1:T(8,128)S(1)}, u32[]{:S(2)}, u32[]{:S(2)}) collective-permute-start(f32[24,14,3,128]{3,0,2,1:T(8,128)S(1)} %get-tuple-element.22), channel_id=1, source_target_pairs={{4,0},{5,1},{6,2},{7,3},{12,8},{13,9},{14,10},{15,11},{20,16},{21,... | collective-permute-start | bytes 1548296 | tf_op jit(solution)/shard_map/ppermute | solution.py:24
  75.8 19.4 %copy-start.7 = (f32[24,14,3,128]{3,0,2,1:T(8,128)}, f32[24,14,3,128]{3,0,2,1:T(8,128)S(1)}, u32[]{:S(2)}) copy-start(f32[24,14,3,128]{3,0,2,1:T(8,128)S(1)} %collective-permute-done.5) | copy-start | bytes 1548292
  79.9 15.2 %copy-start.9 = (f32[24,14,3,128]{3,0,2,1:T(8,128)}, f32[24,14,3,128]{3,0,2,1:T(8,128)S(1)}, u32[]{:S(2)}) copy-start(f32[24,14,3,128]{3,0,2,1:T(8,128)S(1)} %collective-permute-done.6) | copy-start | bytes 1548292
  90.1 16.5 %collective-permute-start.8 = (f32[24,14,14,3]{0,2,3,1:T(8,128)}, f32[24,14,14,3]{0,2,3,1:T(8,128)}, u32[]{:S(2)}, u32[]{:S(2)}) collective-permute-start(f32[24,14,14,3]{0,2,3,1:T(8,128)} %copy.30), channel_id=1, source_target_pairs={{1,0},{2,1},{3,2},{5,4},{6,5},{7,6},{9,8},{10,9},{11,10},{13,12},{... | collective-permute-start | bytes 169352 | tf_op jit(solution)/shard_map/ppermute | solution.py:24
  91.4 13.0 %collective-permute-start.7 = (f32[24,14,14,3]{0,2,3,1:T(8,128)S(1)}, f32[24,14,14,3]{0,2,3,1:T(8,128)}, u32[]{:S(2)}, u32[]{:S(2)}) collective-permute-start(f32[24,14,14,3]{0,2,3,1:T(8,128)S(1)} %copy.28), channel_id=1, source_target_pairs={{0,1},{1,2},{2,3},{4,5},{5,6},{6,7},{8,9},{9,10},{10,11},{12,13},{... | collective-permute-start | bytes 169352 | tf_op jit(solution)/shard_map/ppermute | solution.py:23
  95.4 1.3 %copy-start.1 = (f32[24,14,11,128]{3,0,2,1:T(8,128)}, f32[24,14,11,128]{3,0,2,1:T(8,128)S(1)}, u32[]{:S(2)}) copy-start(f32[24,14,11,128]{3,0,2,1:T(8,128)S(1)} %get-tuple-element.19) | copy-start | bytes 5677060
  95.4 1.9 %copy-start.3 = (f32[24,14,11,128]{3,0,2,1:T(8,128)}, f32[24,14,11,128]{3,0,2,1:T(8,128)S(1)}, u32[]{:S(2)}) copy-start(f32[24,14,11,128]{3,0,2,1:T(8,128)S(1)} %get-tuple-element.20) | copy-start | bytes 5677060
  97.5 0.8 copy-start.14
  99.5 1.4 %copy-start.15 = (f32[3,24,24]{2,1,0:T(8,128)S(1)}, f32[3,24,24]{2,1,0:T(8,128)}, u32[]{:S(2)}) copy-start(f32[3,24,24]{2,1,0:T(8,128)} %param.8) | copy-start | bytes 20740
  113.5 2.6 %copy-start.11 = (f32[8192,24]{0,1:T(8,128)S(1)}, f32[8192,24]{0,1:T(8,128)}, u32[]{:S(2)}) copy-start(f32[8192,24]{0,1:T(8,128)} %fusion.1) | copy-start | bytes 2359300
  113.7 4.7 %copy-start.6 = (f32[24,3,8,128]{3,0,2,1:T(8,128)S(1)}, f32[24,3,8,128]{3,0,2,1:T(8,128)}, u32[]{:S(2)}) copy-start(f32[24,3,8,128]{3,0,2,1:T(8,128)} %copy-done.5) | copy-start | bytes 884740
  113.7 4.7 %copy-start.8 = (f32[24,14,3,128]{3,0,2,1:T(8,128)S(1)}, f32[24,14,3,128]{3,0,2,1:T(8,128)}, u32[]{:S(2)}) copy-start(f32[24,14,3,128]{3,0,2,1:T(8,128)} %copy-done.7) | copy-start | bytes 1548292
  113.7 4.7 %copy-start.10 = (f32[24,14,3,128]{3,0,2,1:T(8,128)S(1)}, f32[24,14,3,128]{3,0,2,1:T(8,128)}, u32[]{:S(2)}) copy-start(f32[24,14,3,128]{3,0,2,1:T(8,128)} %copy-done.9) | copy-start | bytes 1548292
  113.9 4.5 %copy-start.4 = (f32[24,14,11,128]{3,0,2,1:T(8,128)S(1)}, f32[24,14,11,128]{3,0,2,1:T(8,128)}, u32[]{:S(2)}) copy-start(f32[24,14,11,128]{3,0,2,1:T(8,128)} %copy-done.3) | copy-start | bytes 5677060
  116.0 2.4 %copy-start = (f32[24,14,14,3]{3,0,2,1:T(8,128)S(1)}, f32[24,14,14,3]{3,0,2,1:T(8,128)}, u32[]{:S(2)}) copy-start(f32[24,14,14,3]{3,0,2,1:T(8,128)} %copy.31) | copy-start | bytes 169348
  116.0 2.4 %copy-start.2 = (f32[24,14,11,128]{3,0,2,1:T(8,128)S(1)}, f32[24,14,11,128]{3,0,2,1:T(8,128)}, u32[]{:S(2)}) copy-start(f32[24,14,11,128]{3,0,2,1:T(8,128)} %copy-done.1) | copy-start | bytes 5677060
where the time goes:
time: 124 us; the launch traced here: 123 us
  waiting for transfers between devices  49.1 us (40%)
  local copies, waits for them, and re-layouts  27.7 us (22%)
  starting transfers between devices  16.4 us (13%)
  other arithmetic  12.7 us (10%)
  matrix products  10.2 us (8%)
  between operations  6.82 us (6%)
    ppermute x3, waiting for transfers between devices, shifted(): return lax.ppermute(value, axis, pairs)  24.8 us
    ppermute x3, waiting for transfers between devices, padded_2(): before = lax.ppermute(last, axis, up)  15.5 us
    dot_general x6, matrix products, mix_fields(): jnp.dot(matrix, flat, precision=lax.Precision.HIGHEST, preferred_element_...  10.2 us
    ppermute x3, waiting for transfers between devices, padded_2(): after = lax.ppermute(initial, axis, down)  8.84 us
    ppermute x3, starting transfers between devices, padded_2(): before = lax.ppermute(last, axis, up)  8.63 us
    slice x3, local copies, waits for them, and re-layouts, padded_2(): last = lax.slice_in_dim(value, length - width, length, axis=dim)  6.12 us
    div x2, other arithmetic, line_terms(): (-take_at(-2) + 16.0 * take_at(-1) - 30.0 * take_at(0) + 16.0 * take_at(1...  4.25 us
    unnamed x39, local copies, waits for them, and re-layouts  4.14 us
  transfers between devices with their start and end apart: 9, of which 6 were waited for; matrix products, arithmetic and copies ran while one was open for 11% of the time, Pallas kernels for 0%

commit v1 on v0

v1 whole, which is shorter than its diff:
```python
import functools

import jax
import jax.numpy as jnp
from jax import lax
from jax.experimental import pallas as pl
from jax.experimental.pallas import tpu as pltpu
from jax.sharding import PartitionSpec as P

MESH = pl.DeviceIdType.MESH
W = 4
H = 3
SLOT = 8
AXES = ("gx", "gy", "gz")


def roll(value, by):
    return pltpu.roll(value, by % value.shape[-1], value.ndim - 1)


def kernel(
    dims, shift_ref, now_ref, parent_ref, advect_ref, diffuse_ref, slope_ref, value_ref,
    old, box, edge, edge_in, rim, rim_up, rim_low, send_sem, recv_sem,
):
    F, NX, NY, NZ = dims
    cells = NX * NY
    slots = NZ // SLOT
    groups = cells // slots
    me = {a: lax.axis_index(a) for a in AXES}
    size = {a: lax.axis_size(a) for a in AXES}
    below = {a: me[a] > 0 for a in AXES}
    above = {a: me[a] < size[a] - 1 for a in AXES}
    move = [shift_ref[d] for d in range(3)]

    class Copy:
        def __init__(self, n, src, dst, axis, by):
            self.sends = below[axis] if by < 0 else above[axis]
            self.gets = above[axis] if by < 0 else below[axis]
            self.copy = pltpu.make_async_remote_copy(
                src_ref=src, dst_ref=dst, send_sem=send_sem.at[n], recv_sem=recv_sem.at[n],
                device_id={axis: me[axis] + by}, device_id_type=MESH,
            )

        def start(self):
            pl.when(self.sends)(self.copy.start)

        def arrived(self):
            pl.when(self.gets)(self.copy.wait_recv)

        def sent(self):
            pl.when(self.sends)(self.copy.wait_send)

    rim_up[...] = jnp.zeros_like(rim_up)
    rim_low[...] = jnp.zeros_like(rim_low)
    blank = jnp.zeros((F, NZ), jnp.float32)

    def clear_x(y, _):
        for x in (*range(H), *range(NX + H, NX + 2 * H)):
            box[x, y + H] = blank
        return 0

    def clear_y(x, _):
        for y in (*range(H), *range(NY + H, NY + 2 * H)):
            box[x + H, y] = blank
        return 0

    lax.fori_loop(0, NY, clear_x, 0)
    lax.fori_loop(0, NX, clear_y, 0)

    barrier = pltpu.get_barrier_semaphore()
    count = 0
    for a in AXES:
        for cond, by in ((below[a], -1), (above[a], 1)):
            @pl.when(cond)
            def _(a=a, by=by):
                pl.semaphore_signal(
                    barrier, inc=1, device_id={a: me[a] + by}, device_id_type=MESH
                )
        count = count + jnp.where(me[a] > 0, 1, 0) + jnp.where(me[a] < size[a] - 1, 1, 0)

    lane = lax.broadcasted_iota(jnp.int32, (F, NZ), 1)
    slot_of = ((lane + SLOT // 2) % NZ) // SLOT

    def place(g, j):
        k = g * slots + j
        return k, g * (slots // NY) + j // NY, j % NY

    def pack_old(g, _):
        packed = blank
        for j in range(slots):
            k, _, _ = place(g, j)
            row = now_ref[pl.ds(k, F, stride=cells), :]
            packed = jnp.where(slot_of == j, roll(row, SLOT * j), packed)
        edge[g] = packed
        return 0

    lax.fori_loop(0, groups, pack_old, 0)
    pl.semaphore_wait(barrier, count)

    c_edge = Copy(0, edge, edge_in, "gz", -1)
    c_edge.start()
    c_edge.arrived()

    def move_z(g, _):
        for j in range(slots):
            k, x, y = place(g, j)
            row = now_ref[pl.ds(k, F, stride=cells), :]
            tail = roll(edge_in[g], -SLOT * j)
            old[x, y] = pltpu.roll(jnp.where(lane < move[2], tail, row), NZ - move[2], 1)
        return 0

    lax.fori_loop(0, groups, move_z, 0)

    X, Y = pl.ds(0, NX), pl.ds(0, NY)
    half = W // 2
    c_x = Copy(1, old.at[pl.ds(0, W), Y], old.at[pl.ds(NX, W), Y], "gx", -1)
    c_y = Copy(2, old.at[X, pl.ds(0, W)], old.at[X, pl.ds(NY, W)], "gy", -1)
    c_x.start()
    c_y.start()
    c_x.arrived()
    c_cy = Copy(
        3, old.at[pl.ds(NX, half), pl.ds(0, W)], old.at[pl.ds(NX, half), pl.ds(NY, W)], "gy", -1
    )
    c_cy.start()
    c_y.arrived()
    c_cx = Copy(
        4, old.at[pl.ds(half, half), pl.ds(NY, W)],
        old.at[pl.ds(NX + half, half), pl.ds(NY, W)], "gx", -1,
    )
    c_cx.start()
    c_cy.arrived()
    c_cx.arrived()

    in_z = me["gz"] * NZ + lane + move[2] < size["gz"] * NZ

    def move_xy(g, _):
        packed = blank
        for j in range(slots):
            k, x, y = place(g, j)
            in_x = me["gx"] * NX + x + move[0] < size["gx"] * NX
            in_y = me["gy"] * NY + y + move[1] < size["gy"] * NY
            inside = in_z & (in_x & in_y)
            row = jnp.where(
                inside, old[x + move[0], y + move[1]], parent_ref[pl.ds(k, F, stride=cells), :]
            )
            box[x + H, y + H] = row
            packed = jnp.where(slot_of == j, roll(row, SLOT * j), packed)
        rim[g] = packed
        return 0

    lax.fori_loop(0, groups, move_xy, 0)

    BX, BY = pl.ds(H, NX), pl.ds(H, NY)
    halos = [
        Copy(5, box.at[pl.ds(H, H), BY], box.at[pl.ds(NX + H, H), BY], "gx", -1),
        Copy(6, box.at[pl.ds(NX, H), BY], box.at[pl.ds(0, H), BY], "gx", 1),
        Copy(7, box.at[BX, pl.ds(H, H)], box.at[BX, pl.ds(NY + H, H)], "gy", -1),
        Copy(8, box.at[BX, pl.ds(NY, H)], box.at[BX, pl.ds(0, H)], "gy", 1),
        Copy(9, rim, rim_up, "gz", -1),
        Copy(10, rim, rim_low, "gz", 1),
    ]
    for c in halos:
        c.start()
    mats = []
    for a in range(3):
        mats += [advect_ref[a], diffuse_ref[a]]
    matrix = jnp.concatenate(mats, axis=1) / 12.0
    m_high = matrix.astype(jnp.bfloat16)
    m_low = (matrix - m_high.astype(jnp.float32)).astype(jnp.bfloat16)
    for c in halos:
        c.arrived()

    def terms(u, at):
        d1, s1 = at(1) - at(-1), at(1) + at(-1)
        d2, s2 = at(2) - at(-2), at(2) + at(-2)
        s3 = at(3) + at(-3)
        first = 8.0 * d1 - d2
        second = 16.0 * s1 - 30.0 * u - s2
        sixth = s3 - 6.0 * s2 + 15.0 * s1 - 20.0 * u
        return first, second, sixth

    def compute(g, _):
        rims = jnp.where(lane % SLOT < SLOT // 2, rim_up[g], rim_low[g])
        for j0 in range(0, slots, 2):
            columns, us, smooths, ks = [], [], [], []
            for j in (j0, j0 + 1):
                k, x, y = place(g, j)
                u = box[x + H, y + H]
                ends = roll(rims, -SLOT * j)
                z_at = {}
                for o in range(1, H + 1):
                    z_at[o] = roll(jnp.where(lane < o, ends, u), -o)
                    z_at[-o] = roll(jnp.where(lane >= NZ - o, ends, u), o)
                fx, sx, x6 = terms(u, lambda o: box[x + H + o, y + H])
                fy, sy, y6 = terms(u, lambda o: box[x + H, y + H + o])
                fz, sz, z6 = terms(u, lambda o: z_at[o])
                columns.append(jnp.concatenate([fx, sx, fy, sy, fz, sz], axis=0))
                us.append(u)
                smooths.append(x6 + y6 + z6)
                ks.append(k)
            column = jnp.concatenate(columns, axis=1)
            high = column.astype(jnp.bfloat16)
            low = (column - high.astype(jnp.float32)).astype(jnp.bfloat16)
            dot = functools.partial(jnp.dot, preferred_element_type=jnp.float32)
            linear = dot(m_high, high) + (dot(m_low, high) + dot(m_high, low))
            for i in range(2):
                lapse = 1.0 + 0.25 * jnp.tanh(us[i][0:1, :])
                slope = lapse * linear[:, i * NZ:(i + 1) * NZ] + smooths[i] * (1.0 / 64.0)
                slope_ref[pl.ds(ks[i], F, stride=cells), :] = slope
                value_ref[pl.ds(ks[i], F, stride=cells), :] = us[i] + 0.125 * slope
        return 0

    lax.fori_loop(0, groups, compute, 0)

    for c in [c_edge, c_x, c_y, c_cy, c_cx] + halos:
        c.sent()


def local(fields_now, parent, advect, diffuse, box_shift):
    dims = fields_now.shape
    F, NX, NY, NZ = dims
    flat = (F * NX * NY, NZ)
    groups = NX * NY * SLOT // NZ
    edges = pltpu.VMEM((groups, F, NZ), jnp.float32)
    vmem = pl.BlockSpec(memory_space=pltpu.VMEM)
    slope, value = pl.pallas_call(
        functools.partial(kernel, dims),
        out_shape=[jax.ShapeDtypeStruct(flat, jnp.float32)] * 2,
        in_specs=[pl.BlockSpec(memory_space=pltpu.SMEM)] + [vmem] * 4,
        out_specs=[vmem] * 2,
        scratch_shapes=[
            pltpu.VMEM((NX + W, NY + W, F, NZ), jnp.float32),
            pltpu.VMEM((NX + 2 * H, NY + 2 * H, F, NZ), jnp.float32),
            edges, edges, edges, edges, edges,
            pltpu.SemaphoreType.DMA((11,)),
            pltpu.SemaphoreType.DMA((11,)),
        ],
        compiler_params=pltpu.CompilerParams(collective_id=0, has_side_effects=True),
    )(box_shift, fields_now.reshape(flat), parent.reshape(flat), advect, diffuse)
    return slope.reshape(dims), value.reshape(dims)


def solution(mesh):
    return jax.shard_map(
        local,
        mesh=mesh,
        in_specs=(P(None, "gx", "gy", "gz"), P(None, "gx", "gy", "gz"), P(), P(), P()),
        out_specs=(P(None, "gx", "gy", "gz"), P(None, "gx", "gy", "gz")),
        check_vma=False,
    )
```

time: 124 us -> 39.5 us (0.32)
  waiting for transfers between devices: 49.1 us -> 0 us
  Pallas kernels: 0 us -> 35.6 us
  local copies, waits for them, and re-layouts: 27.7 us -> 3.04 us
  starting transfers between devices: 16.4 us -> 0 us
  other arithmetic: 12.7 us -> 0 us
  matrix products: 10.2 us -> 0 us
  between operations: 6.82 us -> 0.65 us
    ppermute x9 -> x0, waiting for transfers between devices: 49.1 us -> none  [the longest x3 24.8 us: shifted(): return lax.ppermute(value, axis, pairs)]
    pallas_call x0 -> x1, Pallas kernels: none -> 35.6 us  [local(): pl.pallas_call(functools.partial(kernel, dims), out_shape=[jax.ShapeDtype...]
    ppermute x9 -> x0, starting transfers between devices: 16.4 us -> none  [the longest x3 8.63 us: padded_2(): before = lax.ppermute(last, axis, up)]
    slice x8 -> x0, local copies, waits for them, and re-layouts: 14.6 us -> none  [the longest x3 6.12 us: padded_2(): last = lax.slice_in_dim(value, length - width, length, axis=dim)]
    dot_general x6 -> x0, matrix products: 10.2 us -> none  [mix_fields(): jnp.dot(matrix, flat, precision=lax.Precision.HIGHEST, preferred_element_...]
    ppermute x3 -> x0, local copies, waits for them, and re-layouts: 7.96 us -> none  [the longest x1 3.61 us: padded_2(): after = lax.ppermute(initial, axis, down)]
    div x3 -> x0, other arithmetic: 4.46 us -> none  [the longest x2 4.25 us: line_terms(): (-take_at(-2) + 16.0 * take_at(-1) - 30.0 * take_at(0) + 16.0 * take_at(1...]
    add x2 -> x0, other arithmetic: 2.41 us -> none  [the longest x1 2.36 us: finish(): section_value = new_box + half_step * section_slope]
  transfers between devices with their start and end apart: 9 -> 0, of which waited for: 6 -> 0; matrix products, arithmetic and copies ran while one was open for 11% -> 0% of each run, Pallas kernels for 0% -> 0%
where the time goes in v1:
time: 39.5 us; the launch traced here: 39.3 us
  Pallas kernels  35.6 us (90%)
  local copies, waits for them, and re-layouts  3.04 us (8%)
  between operations  0.65 us (2%)
    pallas_call x1, Pallas kernels, local(): pl.pallas_call(functools.partial(kernel, dims), out_shape=[jax.ShapeDtype...  35.6 us
    unnamed x4, local copies, waits for them, and re-layouts  3.04 us

profile of v1, /device:TPU:0, one launch (start us, length us, event | category | flops | bytes accessed | tf_op | source)
XLA Modules:
  0.0 39.3 jit_solution(17647199107954850514)
XLA Ops:
  0.6 35.6 %shard_map.68 = (f32[1536,128]{1,0:T(8,128)}, f32[1536,128]{1,0:T(8,128)}) custom-call(s32[3]{0:T(128)} %shift_ref.1, f32[1536,128]{1,0:T(8,128)} %bitcast.4, f32[1536,128]{1,0:T(8,128)} %bitcast.5, f32[3,24,24]{2,1,0:T(8,128)} %advect_ref.1, f32[3,24,24]{2,1,0:T(8,128)} %diffuse_ref.1), custom_call_target="tpu_custom_call" | custom-call | tf_op jit(solution)/shard_map/pallas_call | solution.py:226
  36.3 0.0 copy-start
  36.3 2.2 %copy.9 = f32[24,8,8,128]{3,2,1,0:T(8,128)} copy(f32[24,8,8,128]{3,2,1,0:T(8,128)} %bitcast.7) | data formatting | bytes 1572864
  38.5 0.0 copy-done
  38.5 0.9 %copy.10 = f32[24,8,8,128]{3,2,1,0:T(8,128)} copy(f32[24,8,8,128]{3,2,1,0:T(8,128)S(1)} %bitcast.6) | data formatting | bytes 1572864
Async XLA Ops:
  36.3 2.2 %copy-start = (f32[1536,128]{1,0:T(8,128)S(1)}, f32[1536,128]{1,0:T(8,128)}, u32[]{:S(2)}) copy-start(f32[1536,128]{1,0:T(8,128)} %get-tuple-element.5) | copy-start | bytes 2359300

commit v2 on v1

v2 whole, which is shorter than its diff:
```python
import functools

import jax
import jax.numpy as jnp
from jax import lax
from jax.experimental import pallas as pl
from jax.experimental.pallas import tpu as pltpu
from jax.sharding import PartitionSpec as P

MESH = pl.DeviceIdType.MESH
W = 4
H = 3
SLOT = 8
ROWS = 8
AXES = ("gx", "gy", "gz")


def roll(value, by):
    return pltpu.roll(value, by % value.shape[-1], value.ndim - 1)


def kernel(
    dims, shift_ref, now_hbm, parent_hbm, advect_ref, diffuse_ref, slope_ref, value_ref,
    now_ref, parent_ref, box, edge, edge_in, rim, rim_up, rim_low, mixed, smooth_ref,
    send_sem, recv_sem, load_sem, *old,
):
    F, NX, NY, NZ = dims
    chunks = F // ROWS
    cells = NX * NY
    slots = NZ // SLOT
    groups = cells // slots
    me = {a: lax.axis_index(a) for a in AXES}
    size = {a: lax.axis_size(a) for a in AXES}
    below = {a: me[a] > 0 for a in AXES}
    above = {a: me[a] < size[a] - 1 for a in AXES}
    move = [shift_ref[d] for d in range(3)]
    sems = iter(range(1 + 10 * chunks))

    load_now = pltpu.make_async_copy(now_hbm, now_ref, load_sem.at[0])
    load_parent = pltpu.make_async_copy(parent_hbm, parent_ref, load_sem.at[1])
    load_now.start()
    load_parent.start()

    class Copy:
        def __init__(self, src, dst, axis, by):
            n = next(sems)
            self.sends = below[axis] if by < 0 else above[axis]
            self.gets = above[axis] if by < 0 else below[axis]
            self.copy = pltpu.make_async_remote_copy(
                src_ref=src, dst_ref=dst, send_sem=send_sem.at[n], recv_sem=recv_sem.at[n],
                device_id={axis: me[axis] + by}, device_id_type=MESH,
            )

        def start(self):
            pl.when(self.sends)(self.copy.start)

        def arrived(self):
            pl.when(self.gets)(self.copy.wait_recv)

        def sent(self):
            pl.when(self.sends)(self.copy.wait_send)

    rim_up[...] = jnp.zeros_like(rim_up)
    rim_low[...] = jnp.zeros_like(rim_low)
    blank = jnp.zeros((ROWS, NZ), jnp.float32)

    def clear_x(y, _):
        for c in range(chunks):
            for x in (*range(H), *range(NX + H, NX + 2 * H)):
                box[c, x, y + H] = blank
        return 0

    def clear_y(x, _):
        for c in range(chunks):
            for y in (*range(H), *range(NY + H, NY + 2 * H)):
                box[c, x + H, y] = blank
        return 0

    lax.fori_loop(0, NY, clear_x, 0)
    lax.fori_loop(0, NX, clear_y, 0)

    barrier = pltpu.get_barrier_semaphore()
    count = 0
    for a in AXES:
        for cond, by in ((below[a], -1), (above[a], 1)):
            @pl.when(cond)
            def _(a=a, by=by):
                pl.semaphore_signal(
                    barrier, inc=1, device_id={a: me[a] + by}, device_id_type=MESH
                )
        count = count + jnp.where(me[a] > 0, 1, 0) + jnp.where(me[a] < size[a] - 1, 1, 0)

    lane = lax.broadcasted_iota(jnp.int32, (ROWS, NZ), 1)
    slot_of = ((lane + SLOT // 2) % NZ) // SLOT

    def place(g, j):
        k = g * slots + j
        return k, g * (slots // NY) + j // NY, j % NY

    def rows_of(c, k):
        return pl.ds(c * ROWS * cells + k, ROWS, stride=cells)

    load_now.wait()

    def pack_old(g, _):
        for c in range(chunks):
            packed = blank
            for j in range(slots):
                k, _, _ = place(g, j)
                packed = jnp.where(slot_of == j, roll(now_ref[rows_of(c, k), :], SLOT * j), packed)
            edge[c, g] = packed
        return 0

    lax.fori_loop(0, groups, pack_old, 0)
    pl.semaphore_wait(barrier, count)

    c_edge = Copy(edge, edge_in, "gz", -1)
    c_edge.start()

    X, Y = pl.ds(0, NX), pl.ds(0, NY)
    BX, BY = pl.ds(H, NX), pl.ds(H, NY)
    half = W // 2
    near, far = pl.ds(NX, half), pl.ds(NX + half, half)
    to_x, to_y, corner_y, corner_x, halos = [], [], [], [], []
    for c in range(chunks):
        o, b = old[c], box.at[c]
        to_x.append(Copy(o.at[pl.ds(0, W), Y], o.at[pl.ds(NX, W), Y], "gx", -1))
        to_y.append(Copy(o.at[X, pl.ds(0, W)], o.at[X, pl.ds(NY, W)], "gy", -1))
        corner_y.append(Copy(o.at[near, pl.ds(0, W)], o.at[near, pl.ds(NY, W)], "gy", -1))
        corner_x.append(
            Copy(o.at[pl.ds(half, half), pl.ds(NY, W)], o.at[far, pl.ds(NY, W)], "gx", -1)
        )
        halos.append([
            Copy(b.at[pl.ds(H, H), BY], b.at[pl.ds(NX + H, H), BY], "gx", -1),
            Copy(b.at[pl.ds(NX, H), BY], b.at[pl.ds(0, H), BY], "gx", 1),
            Copy(b.at[BX, pl.ds(H, H)], b.at[BX, pl.ds(NY + H, H)], "gy", -1),
            Copy(b.at[BX, pl.ds(NY, H)], b.at[BX, pl.ds(0, H)], "gy", 1),
            Copy(rim.at[c], rim_up.at[c], "gz", -1),
            Copy(rim.at[c], rim_low.at[c], "gz", 1),
        ])

    def move_z(c):
        def step(g, _):
            for j in range(slots):
                k, x, y = place(g, j)
                tail = roll(edge_in[c, g], -SLOT * j)
                row = jnp.where(lane < move[2], tail, now_ref[rows_of(c, k), :])
                old[c][x, y] = pltpu.roll(row, NZ - move[2], 1)
            return 0

        lax.fori_loop(0, groups, step, 0)

    def send_old(c):
        to_x[c].start()
        to_y[c].start()

    def send_corner(c):
        to_x[c].arrived()
        corner_y[c].start()
        to_y[c].arrived()
        corner_x[c].start()

    in_z = me["gz"] * NZ + lane + move[2] < size["gz"] * NZ

    def move_xy(c):
        corner_y[c].arrived()
        corner_x[c].arrived()

        def step(g, _):
            packed = blank
            for j in range(slots):
                k, x, y = place(g, j)
                in_x = me["gx"] * NX + x + move[0] < size["gx"] * NX
                in_y = me["gy"] * NY + y + move[1] < size["gy"] * NY
                row = jnp.where(
                    in_z & (in_x & in_y),
                    old[c][x + move[0], y + move[1]],
                    parent_ref[rows_of(c, k), :],
                )
                box[c, x + H, y + H] = row
                packed = jnp.where(slot_of == j, roll(row, SLOT * j), packed)
            rim[c, g] = packed
            return 0

        lax.fori_loop(0, groups, step, 0)
        for h in halos[c]:
            h.start()

    def split(value):
        high = value.astype(jnp.bfloat16)
        return high, (value - high.astype(jnp.float32)).astype(jnp.bfloat16)

    def terms(u, at):
        d1, s1 = at(1) - at(-1), at(1) + at(-1)
        d2, s2 = at(2) - at(-2), at(2) + at(-2)
        s3 = at(3) + at(-3)
        first = 8.0 * d1 - d2
        second = 16.0 * s1 - 30.0 * u - s2
        sixth = s3 - 6.0 * s2 + 15.0 * s1 - 20.0 * u
        return first, second, sixth

    def compute(c):
        for h in halos[c]:
            h.arrived()
        fields = slice(c * ROWS, (c + 1) * ROWS)
        mats = [m[a][:, fields] for a in range(3) for m in (advect_ref, diffuse_ref)]
        m_high, m_low = split(jnp.concatenate(mats, axis=1) / 12.0)
        dot = functools.partial(jnp.dot, preferred_element_type=jnp.float32)

        def step(g, _):
            rims = jnp.where(lane % SLOT < SLOT // 2, rim_up[c, g], rim_low[c, g])
            for j0 in range(0, slots, 2):
                columns = []
                for j in (j0, j0 + 1):
                    k, x, y = place(g, j)
                    u = box[c, x + H, y + H]
                    ends = roll(rims, -SLOT * j)
                    z_at = {}
                    for o in range(1, H + 1):
                        z_at[o] = roll(jnp.where(lane < o, ends, u), -o)
                        z_at[-o] = roll(jnp.where(lane >= NZ - o, ends, u), o)
                    fx, sx, x6 = terms(u, lambda o: box[c, x + H + o, y + H])
                    fy, sy, y6 = terms(u, lambda o: box[c, x + H, y + H + o])
                    fz, sz, z6 = terms(u, lambda o: z_at[o])
                    columns.append(jnp.concatenate([fx, sx, fy, sy, fz, sz], axis=0))
                    smooth_ref[c, k] = (x6 + y6 + z6) * (1.0 / 64.0)
                high, low = split(jnp.concatenate(columns, axis=1))
                linear = dot(m_high, high) + (dot(m_low, high) + dot(m_high, low))
                for i in range(2):
                    k = g * slots + j0 + i
                    part = linear[:, i * NZ:(i + 1) * NZ]
                    if c > 0:
                        part = part + mixed[k]
                    if c < chunks - 1:
                        mixed[k] = part
                        continue
                    _, x, y = place(g, j0 + i)
                    lapse = 1.0 + 0.25 * jnp.tanh(box[0, x + H, y + H][0:1, :])
                    for n in range(chunks):
                        slope = lapse * part[n * ROWS:(n + 1) * ROWS] + smooth_ref[n, k]
                        slope_ref[rows_of(n, k), :] = slope
                        value_ref[rows_of(n, k), :] = box[n, x + H, y + H] + 0.125 * slope
            return 0

        lax.fori_loop(0, groups, step, 0)

    c_edge.arrived()
    move_z(0)
    send_old(0)
    for c in range(1, chunks):
        move_z(c)
    load_parent.wait()
    for c in range(chunks):
        if c + 1 < chunks:
            to_x[c].sent()
            to_y[c].sent()
            send_old(c + 1)
        send_corner(c)
        if c > 1:
            compute(c - 2)
        move_xy(c)
    for c in range(max(chunks - 2, 0), chunks):
        compute(c)

    c_edge.sent()
    to_x[-1].sent()
    to_y[-1].sent()
    for c in range(chunks):
        corner_y[c].sent()
        corner_x[c].sent()
        for h in halos[c]:
            h.sent()


def local(fields_now, parent, advect, diffuse, box_shift):
    dims = fields_now.shape
    F, NX, NY, NZ = dims
    flat = (F * NX * NY, NZ)
    chunks = F // ROWS
    groups = NX * NY * SLOT // NZ
    f32 = jnp.float32
    edges = pltpu.VMEM((chunks, groups, ROWS, NZ), f32)
    vmem = pl.BlockSpec(memory_space=pltpu.VMEM)
    hbm = pl.BlockSpec(memory_space=pl.ANY)
    slope, value = pl.pallas_call(
        functools.partial(kernel, dims),
        out_shape=[jax.ShapeDtypeStruct(flat, f32)] * 2,
        in_specs=[pl.BlockSpec(memory_space=pltpu.SMEM), hbm, hbm, vmem, vmem],
        out_specs=[vmem] * 2,
        scratch_shapes=[
            pltpu.VMEM(flat, f32),
            pltpu.VMEM(flat, f32),
            pltpu.VMEM((chunks, NX + 2 * H, NY + 2 * H, ROWS, NZ), f32),
            edges, edges, edges, edges, edges,
            pltpu.VMEM((NX * NY, F, NZ), f32),
            pltpu.VMEM((chunks, NX * NY, ROWS, NZ), f32),
            pltpu.SemaphoreType.DMA((1 + 10 * chunks,)),
            pltpu.SemaphoreType.DMA((1 + 10 * chunks,)),
            pltpu.SemaphoreType.DMA((2,)),
        ] + [pltpu.VMEM((NX + W, NY + W, ROWS, NZ), f32)] * chunks,
        compiler_params=pltpu.CompilerParams(collective_id=0, has_side_effects=True),
    )(box_shift, fields_now.reshape(flat), parent.reshape(flat), advect, diffuse)
    return slope.reshape(dims), value.reshape(dims)


def solution(mesh):
    return jax.shard_map(
        local,
        mesh=mesh,
        in_specs=(P(None, "gx", "gy", "gz"), P(None, "gx", "gy", "gz"), P(), P(), P()),
        out_specs=(P(None, "gx", "gy", "gz"), P(None, "gx", "gy", "gz")),
        check_vma=False,
    )
```

time: 39.5 us -> 39.6 us (level)
  no operation moved by 1% of the time
where the time goes in v2:
time: 39.6 us; the launch traced here: 39.2 us
  Pallas kernels  35.5 us (90%)
  local copies, waits for them, and re-layouts  3.04 us (8%)
  between operations  0.65 us (2%)
    pallas_call x1, Pallas kernels, local(): pl.pallas_call(functools.partial(kernel, dims), out_shape=[jax.ShapeDtype...  35.5 us
    unnamed x4, local copies, waits for them, and re-layouts  3.04 us

profile of v2, /device:TPU:0, one launch (start us, length us, event | category | flops | bytes accessed | tf_op | source)
XLA Modules:
  0.0 39.2 jit_solution(8421286583415589273)
XLA Ops:
  0.6 35.5 %shard_map.68 = (f32[1536,128]{1,0:T(8,128)}, f32[1536,128]{1,0:T(8,128)}) custom-call(s32[3]{0:T(128)} %shift_ref.1, f32[1536,128]{1,0:T(8,128)} %bitcast.4, f32[1536,128]{1,0:T(8,128)} %bitcast.5, f32[3,24,24]{2,1,0:T(8,128)} %advect_ref.1, f32[3,24,24]{2,1,0:T(8,128)} %diffuse_ref.1), custom_call_target="tpu_custom_call" | custom-call | tf_op jit(solution)/shard_map/pallas_call | solution.py:285
  36.1 0.0 copy-start
  36.1 2.2 %copy.9 = f32[24,8,8,128]{3,2,1,0:T(8,128)} copy(f32[24,8,8,128]{3,2,1,0:T(8,128)} %bitcast.7) | data formatting | bytes 1572864
  38.3 0.0 copy-done
  38.3 0.9 %copy.10 = f32[24,8,8,128]{3,2,1,0:T(8,128)} copy(f32[24,8,8,128]{3,2,1,0:T(8,128)S(1)} %bitcast.6) | data formatting | bytes 1572864
Async XLA Ops:
  36.1 2.2 %copy-start = (f32[1536,128]{1,0:T(8,128)S(1)}, f32[1536,128]{1,0:T(8,128)}, u32[]{:S(2)}) copy-start(f32[1536,128]{1,0:T(8,128)} %get-tuple-element.5) | copy-start | bytes 2359300

commit v3 on v2

--- a/solution.py
+++ b/solution.py
@@ -20,9 +20,9 @@
 
 
 def kernel(
-    dims, shift_ref, now_hbm, parent_hbm, advect_ref, diffuse_ref, slope_ref, value_ref,
-    now_ref, parent_ref, box, edge, edge_in, rim, rim_up, rim_low, mixed, smooth_ref,
-    send_sem, recv_sem, load_sem, *old,
+    dims, shift_ref, now_ref, parent_ref, advect_ref, diffuse_ref, slope_ref, value_ref,
+    box, edge, edge_in, rim, rim_up, rim_low, mixed, smooth_ref,
+    send_sem, recv_sem, *old,
 ):
     F, NX, NY, NZ = dims
     chunks = F // ROWS
@@ -34,12 +34,7 @@
     below = {a: me[a] > 0 for a in AXES}
     above = {a: me[a] < size[a] - 1 for a in AXES}
     move = [shift_ref[d] for d in range(3)]
-    sems = iter(range(1 + 10 * chunks))
-
-    load_now = pltpu.make_async_copy(now_hbm, now_ref, load_sem.at[0])
-    load_parent = pltpu.make_async_copy(parent_hbm, parent_ref, load_sem.at[1])
-    load_now.start()
-    load_parent.start()
+    sems = iter(range(11 * chunks))
 
     class Copy:
         def __init__(self, src, dst, axis, by):
@@ -100,22 +95,23 @@
     def rows_of(c, k):
         return pl.ds(c * ROWS * cells + k, ROWS, stride=cells)
 
-    load_now.wait()
-
-    def pack_old(g, _):
-        for c in range(chunks):
+    def pack_old(c):
+        def step(g, _):
             packed = blank
             for j in range(slots):
                 k, _, _ = place(g, j)
                 packed = jnp.where(slot_of == j, roll(now_ref[rows_of(c, k), :], SLOT * j), packed)
             edge[c, g] = packed
-        return 0
-
-    lax.fori_loop(0, groups, pack_old, 0)
-    pl.semaphore_wait(barrier, count)
-
-    c_edge = Copy(edge, edge_in, "gz", -1)
-    c_edge.start()
+            return 0
+
+        lax.fori_loop(0, groups, step, 0)
+
+    edges = [Copy(edge.at[c], edge_in.at[c], "gz", -1) for c in range(chunks)]
+    for c in range(chunks):
+        pack_old(c)
+        if c == 0:
+            pl.semaphore_wait(barrier, count)
+        edges[c].start()
 
     X, Y = pl.ds(0, NX), pl.ds(0, NY)
     BX, BY = pl.ds(H, NX), pl.ds(H, NY)
@@ -140,6 +136,8 @@
         ])
 
     def move_z(c):
+        edges[c].arrived()
+
         def step(g, _):
             for j in range(slots):
                 k, x, y = place(g, j)
@@ -159,6 +157,11 @@
         corner_y[c].start()
         to_y[c].arrived()
         corner_x[c].start()
+
+    def send_halos(c, down):
+        for n, h in enumerate(halos[c]):
+            if (n in (0, 2)) == down:
+                h.start()
 
     in_z = me["gz"] * NZ + lane + move[2] < size["gz"] * NZ
 
@@ -183,8 +186,7 @@
             return 0
 
         lax.fori_loop(0, groups, step, 0)
-        for h in halos[c]:
-            h.start()
+        send_halos(c, False)
 
     def split(value):
         high = value.astype(jnp.bfloat16)
@@ -244,27 +246,30 @@
 
         lax.fori_loop(0, groups, step, 0)
 
-    c_edge.arrived()
     move_z(0)
     send_old(0)
     for c in range(1, chunks):
         move_z(c)
-    load_parent.wait()
-    for c in range(chunks):
+    for c in range(chunks):
+        to_x[c].sent()
+        to_y[c].sent()
         if c + 1 < chunks:
-            to_x[c].sent()
-            to_y[c].sent()
             send_old(c + 1)
-        send_corner(c)
-        if c > 1:
-            compute(c - 2)
-        move_xy(c)
-    for c in range(max(chunks - 2, 0), chunks):
+            send_corner(c)
+        if c > 0:
+            move_xy(c - 1)
+            if c + 1 == chunks:
+                for n in range(c):
+                    send_halos(n, True)
+    last = chunks - 1
+    send_corner(last)
+    move_xy(last)
+    send_halos(last, True)
+    for c in range(chunks):
         compute(c)
 
-    c_edge.sent()
-    to_x[-1].sent()
-    to_y[-1].sent()
+    for c in range(chunks):
+        edges[c].sent()
     for c in range(chunks):
         corner_y[c].sent()
         corner_x[c].sent()
@@ -281,24 +286,22 @@
     f32 = jnp.float32
     edges = pltpu.VMEM((chunks, groups, ROWS, NZ), f32)
     vmem = pl.BlockSpec(memory_space=pltpu.VMEM)
-    hbm = pl.BlockSpec(memory_space=pl.ANY)
     slope, value = pl.pallas_call(
         functools.partial(kernel, dims),
         out_shape=[jax.ShapeDtypeStruct(flat, f32)] * 2,
-        in_specs=[pl.BlockSpec(memory_space=pltpu.SMEM), hbm, hbm, vmem, vmem],
+        in_specs=[pl.BlockSpec(memory_space=pltpu.SMEM)] + [vmem] * 4,
         out_specs=[vmem] * 2,
         scratch_shapes=[
-            pltpu.VMEM(flat, f32),
-            pltpu.VMEM(flat, f32),
             pltpu.VMEM((chunks, NX + 2 * H, NY + 2 * H, ROWS, NZ), f32),
             edges, edges, edges, edges, edges,
             pltpu.VMEM((NX * NY, F, NZ), f32),
             pltpu.VMEM((chunks, NX * NY, ROWS, NZ), f32),
-            pltpu.SemaphoreType.DMA((1 + 10 * chunks,)),
-            pltpu.SemaphoreType.DMA((1 + 10 * chunks,)),
-            pltpu.SemaphoreType.DMA((2,)),
+            pltpu.SemaphoreType.DMA((11 * chunks,)),
+            pltpu.SemaphoreType.DMA((11 * chunks,)),
         ] + [pltpu.VMEM((NX + W, NY + W, ROWS, NZ), f32)] * chunks,
-        compiler_params=pltpu.CompilerParams(collective_id=0, has_side_effects=True),
+        compiler_params=pltpu.CompilerParams(
+            collective_id=0, has_side_effects=True, vmem_limit_bytes=20 * 2**20
+        ),
     )(box_shift, fields_now.reshape(flat), parent.reshape(flat), advect, diffuse)
     return slope.reshape(dims), value.reshape(dims)
 

time: 39.6 us -> 41 us (1.035)
  local copies, waits for them, and re-layouts: 3.04 us -> 6.21 us
  Pallas kernels: 35.5 us -> 33.8 us
    unnamed x4 -> x12, local copies, waits for them, and re-layouts: 3.04 us -> 6.21 us
    pallas_call x1, Pallas kernels: 35.5 us -> 33.8 us  [local(): pl.pallas_call(functools.partial(kernel, dims), out_shape=[jax.ShapeDtype...]
where the time goes in v3:
time: 41 us; the launch traced here: 40.7 us
  Pallas kernels  33.8 us (82%)
  local copies, waits for them, and re-layouts  6.21 us (15%)
  between operations  0.65 us (2%)
    pallas_call x1, Pallas kernels, local(): pl.pallas_call(functools.partial(kernel, dims), out_shape=[jax.ShapeDtype...  33.8 us
    unnamed x12, local copies, waits for them, and re-layouts  6.21 us

profile of v3, /device:TPU:0, one launch (start us, length us, event | category | flops | bytes accessed | tf_op | source)
XLA Modules:
  0.0 40.7 jit_solution(2064081311390252632)
XLA Ops:
  0.6 0.0 copy-start.4
  0.6 0.6 %copy-done.4 = s32[3]{0:T(128)S(1)} copy-done((s32[3]{0:T(128)S(1)}, s32[3]{0:T(128)}, u32[]{:S(2)}) %copy-start.4) | copy-done | bytes 36
  1.3 0.0 copy-start
  1.3 1.1 %copy-done = f32[24,8,8,128]{3,2,1,0:T(8,128)S(1)} copy-done((f32[24,8,8,128]{3,2,1,0:T(8,128)S(1)}, f32[24,8,8,128]{3,2,1,0:T(8,128)}, u32[]{:S(2)}) %copy-start) | copy-done | bytes 786456
  2.4 0.0 copy-start.1
  2.4 1.1 %copy-done.1 = f32[24,8,8,128]{3,2,1,0:T(8,128)S(1)} copy-done((f32[24,8,8,128]{3,2,1,0:T(8,128)S(1)}, f32[24,8,8,128]{3,2,1,0:T(8,128)}, u32[]{:S(2)}) %copy-start.1) | copy-done | bytes 786456
  3.6 0.0 copy-start.2
  3.6 0.8 %copy-done.2 = f32[3,24,24]{2,1,0:T(8,128)S(1)} copy-done((f32[3,24,24]{2,1,0:T(8,128)S(1)}, f32[3,24,24]{2,1,0:T(8,128)}, u32[]{:S(2)}) %copy-start.2) | copy-done | bytes 6936
  4.3 0.0 copy-start.3
  4.3 0.8 %copy-done.3 = f32[3,24,24]{2,1,0:T(8,128)S(1)} copy-done((f32[3,24,24]{2,1,0:T(8,128)S(1)}, f32[3,24,24]{2,1,0:T(8,128)}, u32[]{:S(2)}) %copy-start.3) | copy-done | bytes 6936
  5.1 33.8 %shard_map.68 = (f32[1536,128]{1,0:T(8,128)S(1)}, f32[1536,128]{1,0:T(8,128)S(1)}) custom-call(s32[3]{0:T(128)S(1)} %copy-done.4, f32[1536,128]{1,0:T(8,128)S(1)} %bitcast.4, f32[1536,128]{1,0:T(8,128)S(1)} %bitcast.5, f32[3,24,24]{2,1,0:T(8,128)S(1)} %copy-done.2, f32[3,24,24]{2,1,0:T(8,128)S(1)} %copy-done.3), custom_call_target="tpu_custom_call" | custom-call | tf_op jit(solution)/shard_map/pallas_call | solution.py:289
  38.9 0.9 %copy.9 = f32[24,8,8,128]{3,2,1,0:T(8,128)} copy(f32[24,8,8,128]{3,2,1,0:T(8,128)S(1)} %bitcast.7) | data formatting | bytes 1572864
  39.8 0.9 %copy.10 = f32[24,8,8,128]{3,2,1,0:T(8,128)} copy(f32[24,8,8,128]{3,2,1,0:T(8,128)S(1)} %bitcast.6) | data formatting | bytes 1572864
Async XLA Ops:
  0.6 0.7 %copy-start.4 = (s32[3]{0:T(128)S(1)}, s32[3]{0:T(128)}, u32[]{:S(2)}) copy-start(s32[3]{0:T(128)} %shift_ref.1) | copy-start | bytes 40
  1.3 1.1 %copy-start = (f32[24,8,8,128]{3,2,1,0:T(8,128)S(1)}, f32[24,8,8,128]{3,2,1,0:T(8,128)}, u32[]{:S(2)}) copy-start(f32[24,8,8,128]{3,2,1,0:T(8,128)} %param.5) | copy-start | bytes 2359300
  2.4 1.1 %copy-start.1 = (f32[24,8,8,128]{3,2,1,0:T(8,128)S(1)}, f32[24,8,8,128]{3,2,1,0:T(8,128)}, u32[]{:S(2)}) copy-start(f32[24,8,8,128]{3,2,1,0:T(8,128)} %param.6) | copy-start | bytes 2359300
  3.6 0.8 %copy-start.2 = (f32[3,24,24]{2,1,0:T(8,128)S(1)}, f32[3,24,24]{2,1,0:T(8,128)}, u32[]{:S(2)}) copy-start(f32[3,24,24]{2,1,0:T(8,128)} %advect_ref.1) | copy-start | bytes 20740
  4.3 0.8 %copy-start.3 = (f32[3,24,24]{2,1,0:T(8,128)S(1)}, f32[3,24,24]{2,1,0:T(8,128)}, u32[]{:S(2)}) copy-start(f32[3,24,24]{2,1,0:T(8,128)} %diffuse_ref.1) | copy-start | bytes 20740

commit v4 on v3

--- a/solution.py
+++ b/solution.py
@@ -20,9 +20,9 @@
 
 
 def kernel(
-    dims, shift_ref, now_ref, parent_ref, advect_ref, diffuse_ref, slope_ref, value_ref,
-    box, edge, edge_in, rim, rim_up, rim_low, mixed, smooth_ref,
-    send_sem, recv_sem, *old,
+    dims, shift_hbm, now_hbm, parent_hbm, advect_hbm, diffuse_hbm, slope_ref, value_ref,
+    shift_ref, now_ref, parent_ref, advect_ref, diffuse_ref, box, edge, edge_in, rim, rim_up, rim_low, mixed, smooth_ref,
+    send_sem, recv_sem, load_sem, *old,
 ):
     F, NX, NY, NZ = dims
     chunks = F // ROWS
@@ -33,8 +33,22 @@
     size = {a: lax.axis_size(a) for a in AXES}
     below = {a: me[a] > 0 for a in AXES}
     above = {a: me[a] < size[a] - 1 for a in AXES}
-    move = [shift_ref[d] for d in range(3)]
     sems = iter(range(11 * chunks))
+
+    loads = []
+    span = ROWS * cells
+    for c in range(chunks):
+        part = pl.ds(c * span, span)
+        loads.append(pltpu.make_async_copy(now_hbm.at[part], now_ref.at[part], load_sem.at[c]))
+    loads += [
+        pltpu.make_async_copy(src, dst, load_sem.at[chunks + n])
+        for n, (src, dst) in enumerate((
+            (shift_hbm, shift_ref), (parent_hbm, parent_ref),
+            (advect_hbm, advect_ref), (diffuse_hbm, diffuse_ref),
+        ))
+    ]
+    for n in (0, chunks, *range(1, chunks), *range(chunks + 1, chunks + 4)):
+        loads[n].start()
 
     class Copy:
         def __init__(self, src, dst, axis, by):
@@ -108,6 +122,7 @@
 
     edges = [Copy(edge.at[c], edge_in.at[c], "gz", -1) for c in range(chunks)]
     for c in range(chunks):
+        loads[c].wait()
         pack_old(c)
         if c == 0:
             pl.semaphore_wait(barrier, count)
@@ -134,6 +149,9 @@
             Copy(rim.at[c], rim_up.at[c], "gz", -1),
             Copy(rim.at[c], rim_low.at[c], "gz", 1),
         ])
+
+    loads[chunks].wait()
+    move = [shift_ref[d] for d in range(3)]
 
     def move_z(c):
         edges[c].arrived()
@@ -250,6 +268,8 @@
     send_old(0)
     for c in range(1, chunks):
         move_z(c)
+    for load in loads[chunks + 1:]:
+        load.wait()
     for c in range(chunks):
         to_x[c].sent()
         to_y[c].sent()
@@ -289,18 +309,24 @@
     slope, value = pl.pallas_call(
         functools.partial(kernel, dims),
         out_shape=[jax.ShapeDtypeStruct(flat, f32)] * 2,
-        in_specs=[pl.BlockSpec(memory_space=pltpu.SMEM)] + [vmem] * 4,
+        in_specs=[pl.BlockSpec(memory_space=pltpu.HBM)] * 5,
         out_specs=[vmem] * 2,
         scratch_shapes=[
+            pltpu.SMEM(box_shift.shape, jnp.int32),
+            pltpu.VMEM(flat, f32),
+            pltpu.VMEM(flat, f32),
+            pltpu.VMEM(advect.shape, f32),
+            pltpu.VMEM(diffuse.shape, f32),
             pltpu.VMEM((chunks, NX + 2 * H, NY + 2 * H, ROWS, NZ), f32),
             edges, edges, edges, edges, edges,
             pltpu.VMEM((NX * NY, F, NZ), f32),
             pltpu.VMEM((chunks, NX * NY, ROWS, NZ), f32),
             pltpu.SemaphoreType.DMA((11 * chunks,)),
             pltpu.SemaphoreType.DMA((11 * chunks,)),
+            pltpu.SemaphoreType.DMA((chunks + 4,)),
         ] + [pltpu.VMEM((NX + W, NY + W, ROWS, NZ), f32)] * chunks,
         compiler_params=pltpu.CompilerParams(
-            collective_id=0, has_side_effects=True, vmem_limit_bytes=20 * 2**20
+            collective_id=0, has_side_effects=True
         ),
     )(box_shift, fields_now.reshape(flat), parent.reshape(flat), advect, diffuse)
     return slope.reshape(dims), value.reshape(dims)

time: 41 us -> 38.3 us (0.934)
  local copies, waits for them, and re-layouts: 6.21 us -> 3.04 us
  Pallas kernels: 33.8 us -> 34.5 us
    unnamed x12 -> x4, local copies, waits for them, and re-layouts: 6.21 us -> 3.04 us
    pallas_call x1, Pallas kernels: 33.8 us -> 34.5 us  [local(): pl.pallas_call(functools.partial(kernel, dims), out_shape=[jax.ShapeDtype...]
where the time goes in v4:
time: 38.3 us; the launch traced here: 38.2 us
  Pallas kernels  34.5 us (90%)
  local copies, waits for them, and re-layouts  3.04 us (8%)
  between operations  0.65 us (2%)
    pallas_call x1, Pallas kernels, local(): pl.pallas_call(functools.partial(kernel, dims), out_shape=[jax.ShapeDtype...  34.5 us
    unnamed x4, local copies, waits for them, and re-layouts  3.04 us

profile of v4, /device:TPU:0, one launch (start us, length us, event | category | flops | bytes accessed | tf_op | source)
XLA Modules:
  0.0 38.2 jit_solution(5892753887358299218)
XLA Ops:
  0.6 34.5 %shard_map.68 = (f32[1536,128]{1,0:T(8,128)}, f32[1536,128]{1,0:T(8,128)}) custom-call(s32[3]{0:T(128)} %shift_hbm.1, f32[1536,128]{1,0:T(8,128)} %bitcast.4, f32[1536,128]{1,0:T(8,128)} %bitcast.5, f32[3,24,24]{2,1,0:T(8,128)} %advect_hbm.1, f32[3,24,24]{2,1,0:T(8,128)} %diffuse_hbm.1), custom_call_target="tpu_custom_call" | custom-call | tf_op jit(solution)/shard_map/pallas_call | solution.py:309
  35.1 0.0 copy-start
  35.1 2.2 %copy.9 = f32[24,8,8,128]{3,2,1,0:T(8,128)} copy(f32[24,8,8,128]{3,2,1,0:T(8,128)} %bitcast.7) | data formatting | bytes 1572864
  37.3 0.0 copy-done
  37.3 0.9 %copy.10 = f32[24,8,8,128]{3,2,1,0:T(8,128)} copy(f32[24,8,8,128]{3,2,1,0:T(8,128)S(1)} %bitcast.6) | data formatting | bytes 1572864
Async XLA Ops:
  35.1 2.2 %copy-start = (f32[1536,128]{1,0:T(8,128)S(1)}, f32[1536,128]{1,0:T(8,128)}, u32[]{:S(2)}) copy-start(f32[1536,128]{1,0:T(8,128)} %get-tuple-element.5) | copy-start | bytes 2359300
